TPU v7x, 32 devices: a whole 2x2x4 slice. The times are simulated.
32 devices in a mesh: enc: 4 (over z), grp: 8 (over y, x, core).
Axes of the slice: x: 2, y: 2, z: 4, core: 2. Of those that a mesh axis runs over, the one named last changes fastest.
Arguments:
- patch_feats: bfloat16 [4, 512, 8, 1152], P('enc', 'grp'), may hold values from -6 to 6
- windows: int32 [4, 512, 3, 4], P('enc', 'grp'), may hold values from 0 to 7
- counts: int32 [4, 512], P('enc', 'grp'), may hold values from 1 to 3
- owners: int32 [4, 512], P('enc', 'grp'), may hold values from 0 to 7, as said below
- norm_gain: float32 [1152], replicated, may hold values from 0.1 to 1.9
- norm_bias: float32 [1152], replicated, may hold values from -1.8 to 1.8
- proj_weight: bfloat16 [1152, 4096], replicated, may hold values from -0.1875 to 0.1875
- proj_bias: float32 [4096], replicated, may hold values from -3 to 3
Outputs:
- projected: bfloat16 [4, 1536, 4096], P('enc', 'grp')
Inputs may be any that keep to these rules, and one draw needn't show every extreme that they name: `owners`: within each frame index, each aligned block of 64 clips (the clips of one device) names any section-0 rank at most 8 times, and some rank exactly 8 times.
All inputs are finite; a program needn't handle non-finite values.
Results may differ from a plain program's by a relative error of at most 0.0051.
Values may be sent and summed in bfloat16 or wider, within the bound.
A program may use at most 64 MiB of HBM per device.

v0:
```python
import jax
import jax.numpy as jnp
from jax import lax
from jax.sharding import PartitionSpec as P


def shifted(block, axis, distance):
    devices = range(lax.axis_size(axis))
    route = [(i - distance, i) for i in devices if i - distance in devices]
    return lax.ppermute(block, axis, route)


def pool_frame(frame_feats, frame_windows, norm_gain, norm_bias):
    values = frame_feats.astype(jnp.float32)
    average = jnp.mean(values, axis=-1, keepdims=True)
    spread = jnp.mean((values - average) ** 2, axis=-1, keepdims=True)
    normed = (values - average) * lax.rsqrt(spread + 1e-06) * norm_gain + norm_bias
    patch_ids = jnp.arange(frame_feats.shape[1], dtype=jnp.int32)
    selector = (
        jnp.sum((frame_windows[..., None] == patch_ids).astype(jnp.float32), axis=2)
        / frame_windows.shape[2]
    )
    pooled = jnp.einsum("cst,ctd->csd", selector, normed, precision=lax.Precision.HIGHEST)
    return pooled.astype(jnp.bfloat16)


def shards(patch_feats, windows, counts, owners, norm_gain, norm_bias, proj_weight, proj_bias):
    groups = lax.axis_size("grp")
    width = patch_feats.shape[3]
    pooled = pool_frame(patch_feats[0], windows[0], norm_gain, norm_bias)
    neighbour = shifted(pooled, "enc", -1)
    is_last = lax.axis_index("enc") == lax.axis_size("enc") - 1
    following = jnp.where(is_last, pooled, neighbour)
    merged = ((pooled.astype(jnp.float32) + following.astype(jnp.float32)) * 0.5).astype(
        jnp.bfloat16
    )
    samples = pooled.shape[0]
    per_sample = pooled.shape[1]
    most_per = -(-samples // groups)
    slot_rows = most_per * per_sample
    rows_out = groups * slot_rows
    count_row = counts[0]
    owner_row = owners[0]
    rank_ids = jnp.arange(groups, dtype=jnp.int32)
    matches = (owner_row[:, None] == rank_ids[None, :]).astype(jnp.int32)
    weighted = matches * count_row[:, None]
    earlier = jnp.cumsum(weighted, axis=0) - weighted
    within = jnp.sum(earlier * matches, axis=1)
    totals = jnp.sum(weighted, axis=0)
    step_index = jnp.arange(per_sample, dtype=jnp.int32)
    is_valid = step_index[None, :] < count_row[:, None]
    target = owner_row[:, None] * slot_rows + within[:, None] + step_index[None, :]
    target = jnp.where(is_valid, target, rows_out)
    token_ids = jnp.arange(samples * per_sample, dtype=jnp.int32)
    source = (
        jnp.full((rows_out + 1,), samples * per_sample, jnp.int32)
        .at[target.reshape(-1)]
        .set(token_ids)[:rows_out]
    )
    local_rows = merged.reshape(-1, width)
    row_width = local_rows.shape[1]
    flat_rows = jnp.concatenate([local_rows, jnp.zeros((1, row_width), jnp.bfloat16)], axis=0)
    outgoing = jnp.take(flat_rows, source, axis=0).reshape(groups, slot_rows, row_width)
    row_index = jnp.arange(rows_out, dtype=jnp.int32)
    received, arrived = (
        lax.all_to_all(outgoing, "grp", split_axis=0, concat_axis=0, tiled=True),
        lax.all_to_all(totals.reshape(groups, 1), "grp", split_axis=0, concat_axis=0, tiled=True),
    )
    arrived = arrived[:, 0]
    ending = jnp.cumsum(arrived)
    opening = ending - arrived
    sender = jnp.sum((ending[None, :] <= row_index[:, None]).astype(jnp.int32), axis=1)
    sender = jnp.minimum(sender, groups - 1)
    is_live = row_index < ending[-1]
    picked = sender * slot_rows + row_index - jnp.take(opening, sender)
    source_rows = jnp.where(is_live, picked, rows_out).astype(jnp.int32)
    gathered_rows = jnp.concatenate(
        [received.reshape(rows_out, row_width), jnp.zeros((1, row_width), jnp.bfloat16)], axis=0
    )
    packed = jnp.take(gathered_rows, source_rows, axis=0)
    product = jnp.dot(packed, proj_weight, preferred_element_type=jnp.float32)
    result = jnp.where(is_live[:, None], product + proj_bias, 0.0).astype(jnp.bfloat16)
    return result[None]


def solution(mesh):
    placed = (
        P("enc", "grp", None, None),
        P("enc", "grp", None, None),
        P("enc", "grp"),
        P("enc", "grp"),
        P(),
        P(),
        P(),
        P(),
    )
    return jax.shard_map(
        shards, mesh=mesh, in_specs=placed, out_specs=P("enc", "grp", None), check_vma=False
    )
```

profile of v0, /device:TPU:0, one launch (start us, length us, event | category | flops | bytes accessed | tf_op | source)
XLA Modules:
  0.0 52.7 jit_solution(15215078467456572550)
XLA Ops:
  0.0 0.8 %fusion.17 = s32[64,8]{1,0:T(8,128)S(1)} fusion(s32[64]{0:T(128)} %bitcast.44, s32[64]{0:T(128)} %bitcast.50), kind=kLoop, calls=%fused_computation.33 | loop fusion | flops 1024 | bytes 2560 | tf_op jit(solution)/shard_map/mul | solution.py:46
  0.9 0.1 reduce_window_sum.18
  1.0 0.9 %select_reduce_fusion = (s32[64]{0:T(128)S(1)}, s32[8]{0:T(128)S(1)}) fusion(s32[64,8]{1,0:T(8,128)S(1)} %reduce_window_sum.18, s32[64]{0:T(128)} %bitcast.45, s32[64]{0:T(128)} %bitcast.51), kind=kLoop, calls=%fused_computation.29 | loop fusion | flops 3000 | bytes 2848 | tf_op jit(solution)/shard_map/reduce_sum | solution.py:48
  1.8 0.7 %copy.19 = s32[8,1,1]{2,1,0:T(1,128)} copy(s32[8,1,1]{0,2,1:T(1,128)S(1)} %bitcast.52) | data formatting | bytes 64 | tf_op jit(solution)/shard_map/all_to_all | solution.py:67
  2.5 5.2 %all-to-all-start = ((s32[8,1,1]{2,1,0:T(1,128)}), s32[8,1,1]{2,1,0:T(1,128)S(1)}, u32[]{:S(2)}, u32[]{:S(2)}) async-start(s32[8,1,1]{2,1,0:T(1,128)} %copy.19), calls=%async_computation | async-start | bytes 8192 | tf_op jit(solution)/shard_map/all_to_all | solution.py:67
  7.7 0.7 %convert_reduce_fusion.1 = f32[64,3,8]{0,2,1:T(8,128)S(1)} fusion(s32[64,3,4]{0,2,1:T(4,128)} %bitcast.43), kind=kLoop, calls=%fused_computation.26 | loop fusion | flops 16896 | bytes 9216 | tf_op jit(solution)/shard_map/reduce_sum | solution.py:20
  8.4 1.5 %convert_reduce_fusion = f32[64,8]{1,0:T(8,128)S(1)} fusion(bf16[1,64,8,1152]{3,2,1,0:T(8,128)(2,1)} %param.10), kind=kLoop, calls=%fused_computation.7 | loop fusion | flops 1179136 | bytes 1181696 | tf_op jit(solution)/shard_map/reduce_sum | solution.py:15
  9.9 1.7 %fusion.6 = f32[64,8]{1,0:T(8,128)S(1)} fusion(bf16[1,64,8,1152]{3,2,1,0:T(8,128)(2,1)} %param.10, f32[64,8]{1,0:T(8,128)S(1)} %broadcast_multiply_fusion), kind=kLoop, calls=%fused_computation.13 | loop fusion | flops 2358784 | bytes 1183744 | tf_op jit(solution)/shard_map/reduce_sum | solution.py:16
  11.7 0.0 copy-start.1
  11.7 0.1 copy.20
  11.8 2.5 %convolution_convert_fusion = bf16[64,3,1152]{2,1,0:T(4,128)(2,1)S(1)} fusion(f32[64,3,8]{2,1,0:T(4,128)S(1)} %copy.20, bf16[1,64,8,1152]{3,2,1,0:T(8,128)(2,1)S(1)} %copy-done, f32[1152]{0:T(1024)S(1)} %copy-done.4, f32[1152]{0:T(1024)S(1)} %copy-done.5, f32[64,8]{1,0:T(8,128)S(1)} %add_rsqrt_fusion, f32[64,8]{1,0:T(8,128)S(1)} %broadcast_multiply_fusion), kind=kOutput, calls=%fused_computation.9 | convolution fusion | flops 24403968 | bytes 1641472 | tf_op jit(solution)/shard_map/cst,ctd->csd/dot_general | solution.py:23
  14.4 1.3 %collective-permute-start = (bf16[64,3,1152]{2,0,1:T(8,128)(2,1)S(1)}, bf16[64,3,1152]{2,0,1:T(8,128)(2,1)S(1)}, u32[]{:S(2)}, u32[]{:S(2)}) collective-permute-start(bf16[64,3,1152]{2,0,1:T(8,128)(2,1)S(1)} %copy.21), channel_id=1, source_target_pairs={{8,0},{16,8},{24,16},{9,1},{17,9},{25,17},{10,2},{18,10},{26,18},{... | collective-permute-start | bytes 1327112 | tf_op jit(solution)/shard_map/ppermute | solution.py:10
  15.7 0.1 add_select_fusion
  15.8 0.1 select_n.70
  16.0 1.2 %scatter_custom_fusion = s32[193]{0:T(256)S(1)} fusion(s32[192]{0:T(256)S(1)} %bitcast.53, s32[192]{0:T(256)S(1)} %iota.27, s32[]{:T(128)} %constant.38.clone.1), kind=kCustom, calls=%fused_computation.61 | custom fusion | bytes 776 | tf_op jit(solution)/shard_map/scatter | solution.py:58
  17.2 0.0 all-to-all-done
  17.3 0.2 reduce.1
  17.5 0.2 reduce-window.4
  17.7 0.1 convert_reduce_fusion.2
  17.8 0.7 %fusion.24 = (s32[1]{0:T(128)}, s32[1]{0:T(128)}, s32[1]{0:T(128)}, s32[1]{0:T(128)}, s32[1]{0:T(128)}, /*index=5*/s32[1]{0:T(128)}, s32[1]{0:T(128)}, s32[1]{0:T(128)}) fusion(s32[8]{0:T(128)S(1)} %bitcast_subtract_fusion), kind=kLoop, calls=%fused_computation.65 | loop fusion | bytes 64 | tf_op jit(solution)/shard_map/jit(_take)/gather | solution.py:75
  18.5 4.3 %compare_select_fusion.4 = s32[192,1]{0,1:T(1,128)S(1)} fusion(s32[]{:T(128)} %bitcast.7, s32[]{:T(128)} %bitcast.8, s32[]{:T(128)} %bitcast.9, s32[]{:T(128)} %bitcast.10, s32[]{:T(128)} %bitcast.11, s32[]{:T(128)} %bitcast.13, s32[]{:T(128)} %bitcast.12, s32[192,1]{0,1:T(1,128)S(1)} %bitcast.47), kind=kLoop, calls=%fused_computation.46 | loop fusion | flops 2880 | bytes 1564 | tf_op jit(solution)/shard_map/jit(_take)/gather | solution.py:75
  22.7 6.1 %collective-permute-done = bf16[64,3,1152]{2,0,1:T(8,128)(2,1)S(1)} collective-permute-done((bf16[64,3,1152]{2,0,1:T(8,128)(2,1)S(1)}, bf16[64,3,1152]{2,0,1:T(8,128)(2,1)S(1)}, u32[]{:S(2)}, u32[]{:S(2)}) %collective-permute-start) | collective-permute-done | bytes 442400 | tf_op jit(solution)/shard_map/ppermute | solution.py:10
  28.9 0.5 %multiply_convert_fusion = bf16[64,3,1152]{2,1,0:T(4,128)(2,1)S(1)} fusion(bf16[64,3,1152]{2,1,0:T(4,128)(2,1)S(1)} %convolution_convert_fusion, bf16[64,3,1152]{2,0,1:T(8,128)(2,1)S(1)} %collective-permute-done, pred[]{:T(512)S(6)} %eq.41), kind=kLoop, calls=%fused_computation.16 | loop fusion | flops 1327104 | bytes 1327105 | tf_op jit(solution)/shard_map/convert_element_type | solution.py:34
  29.4 0.4 reshape.138
  29.8 1.1 %gather_fusion = bf16[192,1152]{1,0:T(8,128)(2,1)S(1)} fusion(bf16[193,1152]{1,0:T(8,128)(2,1)S(1)} %concatenate.6, s32[1024]{0:T(1024)S(1)} %pad_clamp_fusion.1), kind=kCustom, calls=%fused_computation.clone | custom fusion | bytes 885504 | tf_op jit(solution)/shard_map/jit(_take)/gather | solution.py:63
  30.9 0.9 %broadcast_select_fusion = bf16[192,1152]{1,0:T(8,128)(2,1)} fusion(bf16[192,1152]{1,0:T(8,128)(2,1)S(1)} %gather_fusion, pred[192]{0:T(512)(128)(4,1)S(1)} %compare_and_fusion.1), kind=kLoop, calls=%fused_computation.24 | loop fusion | flops 221184 | bytes 884928 | tf_op jit(solution)/shard_map/jit(_take)/select_n | solution.py:63
  31.8 3.8 %all-to-all-start.1 = ((bf16[8,24,1152]{2,1,0:T(8,128)(2,1)}), bf16[8,24,1152]{2,1,0:T(8,128)(2,1)S(1)}, u32[]{:S(2)}, u32[]{:S(2)}) async-start(bf16[8,24,1152]{2,1,0:T(8,128)(2,1)} %bitcast.18), calls=%async_computation.1 | async-start | bytes 884736 | tf_op jit(solution)/shard_map/all_to_all | solution.py:66
  35.7 0.6 %slice.7 = s32[1,1]{0,1:T(1,128)} slice(s32[8,1]{0,1:T(1,128)S(1)} %reduce-window.4), slice={[7:8], [0:1]} | slice | bytes 8 | tf_op jit(solution)/shard_map/slice | solution.py:74
  36.2 1.3 %compare_and_fusion = (pred[192]{0:T(512)(128)(4,1)S(1)}, s32[192]{0:T(256)S(1)}, pred[192]{0:T(512)(128)(4,1)S(1)}) fusion(pred[192]{0:T(512)(128)(4,1)S(1)} %compare_reduce_fusion, s32[192]{0:T(256)S(1)} %bitcast.49, s32[]{:T(128)} %bitcast.6, s32[192]{0:T(256)S(1)} %convert_reduce_fusion.2, s32[]{:T(128)} %bitcast.3), kind=kLoop, calls=%fused_computation.53 | loop fusion | flops 3840 | bytes 2888 | tf_op jit(solution)/shard_map/jit(_take)/and | solution.py:80
  37.5 7.0 %all-to-all-done.1 = bf16[8,24,1152]{2,1,0:T(8,128)(2,1)S(1)} async-done(((bf16[8,24,1152]{2,1,0:T(8,128)(2,1)}), bf16[8,24,1152]{2,1,0:T(8,128)(2,1)S(1)}, u32[]{:S(2)}, u32[]{:S(2)}) %all-to-all-start.1) | async-done | bytes 442400 | tf_op jit(solution)/shard_map/all_to_all | solution.py:66
  44.5 1.1 %gather_fusion.1 = bf16[192,1152]{1,0:T(8,128)(2,1)S(1)} fusion(bf16[193,1152]{1,0:T(8,128)(2,1)S(1)} %concatenate.7, s32[1024]{0:T(1024)S(1)} %pad_clamp_fusion), kind=kCustom, calls=%fused_computation.1.clone | custom fusion | bytes 885504 | tf_op jit(solution)/shard_map/jit(_take)/gather | solution.py:80
  45.6 7.1 %fusion.2 = bf16[1,192,4096]{2,1,0:T(8,128)(2,1)} fusion(bf16[1152,4096]{1,0:T(8,128)(2,1)} %param.16, f32[4096]{0:T(1024)S(1)} %copy-done.3, pred[192]{0:T(512)(128)(4,1)S(1)} %get-tuple-element.18, bf16[192,1152]{1,0:T(8,128)(2,1)S(1)} %gather_fusion.1, pred[192]{0:T(512)(128)(4,1)S(1)} %get-tuple-element.8), kind=kOutput, calls=%fused_computation.6 | convolution fusion | flops 1814519808 | bytes 11469184 | tf_op jit(solution)/shard_map/dot_general | solution.py:81
  (27 shorter events, 0.2 us)
Async XLA Ops:
  0.0 11.8 %copy-start = (bf16[1,64,8,1152]{3,2,1,0:T(8,128)(2,1)S(1)}, bf16[1,64,8,1152]{3,2,1,0:T(8,128)(2,1)}, u32[]{:S(2)}) copy-start(bf16[1,64,8,1152]{3,2,1,0:T(8,128)(2,1)} %param.10) | copy-start | bytes 3538948
  0.0 11.8 %copy-start.4 = (f32[1152]{0:T(1024)S(1)}, f32[1152]{0:T(1024)}, u32[]{:S(2)}) copy-start(f32[1152]{0:T(1024)} %param.15) | copy-start | bytes 13828
  0.0 11.8 %copy-start.5 = (f32[1152]{0:T(1024)S(1)}, f32[1152]{0:T(1024)}, u32[]{:S(2)}) copy-start(f32[1152]{0:T(1024)} %param.14) | copy-start | bytes 13828
  2.5 14.7 %all-to-all-start = ((s32[8,1,1]{2,1,0:T(1,128)}), s32[8,1,1]{2,1,0:T(1,128)S(1)}, u32[]{:S(2)}, u32[]{:S(2)}) async-start(s32[8,1,1]{2,1,0:T(1,128)} %copy.19), calls=%async_computation | async-start | bytes 8192 | tf_op jit(solution)/shard_map/all_to_all | solution.py:67
  11.7 4.1 %copy-start.2 = (s32[1,64]{1,0:T(1,128)S(1)}, s32[1,64]{1,0:T(1,128)}, u32[]{:S(2)}) copy-start(s32[1,64]{1,0:T(1,128)} %param.13) | copy-start | bytes 772
  11.7 4.1 %copy-start.1 = (s32[1,64]{1,0:T(1,128)S(1)}, s32[1,64]{1,0:T(1,128)}, u32[]{:S(2)}) copy-start(s32[1,64]{1,0:T(1,128)} %param.12) | copy-start | bytes 772
  14.4 14.5 %collective-permute-start = (bf16[64,3,1152]{2,0,1:T(8,128)(2,1)S(1)}, bf16[64,3,1152]{2,0,1:T(8,128)(2,1)S(1)}, u32[]{:S(2)}, u32[]{:S(2)}) collective-permute-start(bf16[64,3,1152]{2,0,1:T(8,128)(2,1)S(1)} %copy.21), channel_id=1, source_target_pairs={{8,0},{16,8},{24,16},{9,1},{17,9},{25,17},{10,2},{18,10},{26,18},{... | collective-permute-start | bytes 1327112 | tf_op jit(solution)/shard_map/ppermute | solution.py:10
  31.8 12.6 %all-to-all-start.1 = ((bf16[8,24,1152]{2,1,0:T(8,128)(2,1)}), bf16[8,24,1152]{2,1,0:T(8,128)(2,1)S(1)}, u32[]{:S(2)}, u32[]{:S(2)}) async-start(bf16[8,24,1152]{2,1,0:T(8,128)(2,1)} %bitcast.18), calls=%async_computation.1 | async-start | bytes 884736 | tf_op jit(solution)/shard_map/all_to_all | solution.py:66
  44.5 1.1 %copy-start.3 = (f32[4096]{0:T(1024)S(1)}, f32[4096]{0:T(1024)}, u32[]{:S(2)}) copy-start(f32[4096]{0:T(1024)} %param.17) | copy-start | bytes 49156
where the time goes:
time: 53.2 us; the launch traced here: 52.7 us
  other arithmetic  13.3 us (25%)
  waiting for transfers between devices  13.1 us (25%)
  starting transfers between devices  10.3 us (19%)
  matrix products  9.63 us (18%)
  local copies, waits for them, and re-layouts  6.08 us (11%)
    dot_general x1, matrix products, shards(): product = jnp.dot(packed, proj_weight, preferred_element_type=jnp.float32)  7.11 us
    all_to_all x1, waiting for transfers between devices, shards(): lax.all_to_all(outgoing, 'grp', split_axis=0, concat_axis=0, tiled=True)  6.96 us
    ppermute x1, waiting for transfers between devices, shifted(): return lax.ppermute(block, axis, route)  6.14 us
    all_to_all x1, starting transfers between devices, shards(): lax.all_to_all(totals.reshape(groups, 1), 'grp', split_axis=0, concat_axi...  5.2 us
    gather x2, other arithmetic, shards(): picked = sender * slot_rows + row_index - jnp.take(opening, sender)  4.28 us
    all_to_all x1, starting transfers between devices, shards(): lax.all_to_all(outgoing, 'grp', split_axis=0, concat_axis=0, tiled=True)  3.81 us
    dot_general x1, matrix products, pool_frame(): jnp.einsum('cst,ctd->csd', selector, normed, precision=lax.Precision.HIGH...  2.52 us
    reduce_sum x1, other arithmetic, pool_frame(): spread = jnp.mean((values - average) ** 2, axis=-1, keepdims=True)  1.71 us
  transfers between devices with their start and end apart: 3, of which 2 were waited for; matrix products, arithmetic and copies ran while one was open for 29% of the time, Pallas kernels for 0%

commit v1 on v0

v1 whole, which is shorter than its diff:
```python
import functools

import jax
import jax.numpy as jnp
from jax import lax
from jax.experimental import pallas as pl
from jax.experimental.pallas import tpu as pltpu
from jax.sharding import PartitionSpec as P

MESH = pl.DeviceIdType.MESH
F32 = jnp.float32
BF16 = jnp.bfloat16


def partner(me, k, groups):
    if groups & (groups - 1):
        return (me + k) % groups
    total, bit = 0, 1
    while bit < groups:
        total = total + (me // bit + k // bit) % 2 * bit
        bit *= 2
    return total


def iota(shape, axis):
    return lax.broadcasted_iota(jnp.int32, shape, axis)


def to_column(row):
    n = row.shape[1]
    return jnp.sum(jnp.where(iota((n, n), 0) == iota((n, n), 1), row, 0.0), axis=1, keepdims=True)


def placements(count_row, owner_row, rows, slot, per_sample):
    counts, owners = count_row.astype(F32), owner_row.astype(F32)
    n = counts.shape[1]
    same = (to_column(owners) == owners) & (iota((n, n), 0) < iota((n, n), 1))
    start = jnp.sum(jnp.where(same, to_column(counts), 0.0), axis=0, keepdims=True)
    first = owners * slot + start
    row_ids = iota((rows, n), 0).astype(F32)
    return [
        (row_ids == jnp.where(counts > t, first + t, -1.0)).astype(F32).astype(BF16)
        for t in range(per_sample)
    ]


def kernel(
    groups, frames, per_sample, patches, slot,
    feats_ref, win_ref, cnt_ref, own_ref, gain_ref, bias_ref,
    packed_ref, live_ref,
    normed, pooled, zsend, zrecv, outgoing, arrived,
    all_cnt, all_own, prev_cnt, prev_own,
    z_send, z_recv, a_send, a_recv, c_send, c_recv, o_send, o_recv,
):
    frame, me = lax.axis_index("enc"), lax.axis_index("grp")
    first, last = frame == 0, frame == frames - 1
    width = feats_ref.shape[1]
    clips = cnt_ref.shape[1]
    rows = groups * slot
    order = list(range(groups - 1, -1, -1))

    barrier = pltpu.get_barrier_semaphore()
    for k in order[:-1]:
        pl.semaphore_signal(
            barrier, inc=1, device_id=(frame, partner(me, k, groups)), device_id_type=MESH
        )

    @pl.when(jnp.logical_not(first))
    def _():
        pl.semaphore_signal(barrier, inc=1, device_id=(frame - 1, me), device_id_type=MESH)

    @pl.when(jnp.logical_not(last))
    def _():
        pl.semaphore_signal(barrier, inc=1, device_id=(frame + 1, me), device_id_type=MESH)

    step_rows = 32
    gain, bias = gain_ref[...], bias_ref[...]

    def norm_step(i):
        at = pl.ds(pl.multiple_of(i * step_rows, step_rows), step_rows)
        values = feats_ref[at, :].astype(F32)
        centred = values - jnp.sum(values, axis=1, keepdims=True) * (1.0 / width)
        spread = jnp.sum(centred * centred, axis=1, keepdims=True) * (1.0 / width)
        normed[at, :] = (centred * lax.rsqrt(spread + 1e-06) * gain + bias).astype(BF16)

    steps = feats_ref.shape[0] // step_rows
    early = steps // 4
    pl.loop(0, early)(norm_step)

    neighbours = (frame + frames - 1) // frames + (2 * (frames - 1) - frame) // frames
    pl.semaphore_wait(barrier, groups - 1 + neighbours)

    def remote(src, dst, send, recv, k, device):
        return pltpu.make_async_remote_copy(
            src_ref=src, dst_ref=dst, send_sem=send.at[k], recv_sem=recv.at[k],
            device_id=device, device_id_type=MESH,
        )

    def enc_meta():
        to = (frame + 1, me)
        return (
            remote(cnt_ref, prev_cnt, c_send, c_recv, 0, to),
            remote(own_ref, prev_own, o_send, o_recv, 0, to),
        )

    def grp_meta(k):
        to = (frame, partner(me, k, groups))
        return (
            remote(cnt_ref, all_cnt.at[me], c_send, c_recv, k, to),
            remote(own_ref, all_own.at[me], o_send, o_recv, k, to),
        )

    def z_copy(k):
        o = partner(me, k, groups)
        return remote(zsend.at[o], zrecv.at[o], z_send, z_recv, k, (frame - 1, me))

    def a_copy(k):
        o = partner(me, k, groups)
        return remote(outgoing.at[o], arrived.at[me], a_send, a_recv, k, (frame, o))

    @pl.when(jnp.logical_not(last))
    def _():
        for copy in enc_meta():
            copy.start()

    for k in order[:-1]:
        for copy in grp_meta(k):
            copy.start()
    all_cnt[me] = cnt_ref[...]
    all_own[me] = own_ref[...]

    pl.loop(early, steps)(norm_step)

    cells = clips * patches
    cell_ids = iota((clips, cells), 1)
    base = iota((clips, 1), 0) * patches
    members = win_ref.shape[1]
    eye = (iota((clips, clips), 0) == iota((clips, clips), 1)).astype(F32).astype(BF16)
    for t in range(per_sample):
        picks = lax.dot_general(
            eye,
            win_ref[t].astype(F32).astype(BF16),
            (((1,), (1,)), ((), ())),
            preferred_element_type=F32,
        ).astype(jnp.int32)
        chosen = jnp.zeros((clips, cells), F32)
        for w in range(members):
            chosen += (cell_ids == base + picks[:, w : w + 1]).astype(F32)
        total = jnp.dot(chosen.astype(BF16), normed[...], preferred_element_type=F32)
        pooled[t] = (total * (1.0 / members)).astype(BF16)

    def sort_rows(count_row, owner_row):
        total = jnp.zeros((rows, width), F32)
        for t, chosen in enumerate(placements(count_row, owner_row, rows, slot, per_sample)):
            total += jnp.dot(chosen, pooled[t], preferred_element_type=F32)
        return total.astype(BF16).reshape(groups, slot, width)

    @pl.when(jnp.logical_not(first))
    def _():
        for copy in enc_meta():
            copy.wait_recv()
        zsend[...] = sort_rows(prev_cnt[...], prev_own[...])
        for k in order:
            z_copy(k).start()

    outgoing[...] = sort_rows(cnt_ref[...], own_ref[...])

    for k in order:
        o = partner(me, k, groups)

        @pl.when(jnp.logical_not(last))
        def _():
            z_copy(k).wait_recv()
            outgoing[o] = ((outgoing[o].astype(F32) + zrecv[o].astype(F32)) * 0.5).astype(BF16)

        if k:
            a_copy(k).start()
        else:
            arrived[me] = outgoing[me]

    lane = iota((1, rows), 1)
    opening, size = jnp.zeros((1, rows), F32), jnp.zeros((1, rows), F32)
    amount = jnp.zeros((1, 1), F32)
    for k in order[:-1]:
        for copy in grp_meta(k):
            copy.wait_recv()
    for s in range(groups):
        mine = all_own[s] == me
        sent = jnp.sum(jnp.where(mine, all_cnt[s], 0).astype(F32), axis=1, keepdims=True)
        opening += jnp.where(lane // slot > s, sent, 0.0)
        size += jnp.where(lane // slot == s, sent, 0.0)
        amount += sent
    within = (lane % slot).astype(F32)
    target = jnp.where(within < size, opening + within, -1.0)
    rows_out = packed_ref.shape[0]
    chosen = (iota((rows_out, rows), 0).astype(F32) == target).astype(F32).astype(BF16)
    live_ref[...] = (iota((rows_out, 1), 0).astype(F32) < amount).astype(F32)

    for k in order[:-1]:
        a_copy(k).wait_recv()
    packed_ref[...] = jnp.dot(
        chosen, arrived[...].reshape(rows, width), preferred_element_type=F32
    ).astype(BF16)

    for k in order[:-1]:
        a_copy(k).wait_send()
        for copy in grp_meta(k):
            copy.wait_send()

    @pl.when(jnp.logical_not(first))
    def _():
        for k in order:
            z_copy(k).wait_send()

    @pl.when(jnp.logical_not(last))
    def _():
        for copy in enc_meta():
            copy.wait_send()


def shards(patch_feats, windows, counts, owners, norm_gain, norm_bias, proj_weight, proj_bias):
    groups, frames = lax.axis_size("grp"), lax.axis_size("enc")
    _, clips, patches, width = patch_feats.shape
    per_sample = windows.shape[2]
    slot_rows = -(-clips // groups) * per_sample
    slot = -(-slot_rows // 8) * 8
    rows_out = groups * slot_rows
    block = (groups, slot, width)
    dma = pltpu.SemaphoreType.DMA((groups,))
    packed, live = pl.pallas_call(
        functools.partial(kernel, groups, frames, per_sample, patches, slot),
        out_shape=(
            jax.ShapeDtypeStruct((rows_out, width), BF16),
            jax.ShapeDtypeStruct((rows_out, 1), F32),
        ),
        in_specs=[pl.BlockSpec(memory_space=pltpu.VMEM)] * 6,
        out_specs=[pl.BlockSpec(memory_space=pltpu.VMEM)] * 2,
        scratch_shapes=[
            pltpu.VMEM((clips * patches, width), BF16),
            pltpu.VMEM((per_sample, clips, width), BF16),
            pltpu.VMEM(block, BF16),
            pltpu.VMEM(block, BF16),
            pltpu.VMEM(block, BF16),
            pltpu.VMEM(block, BF16),
            pltpu.VMEM((groups, 1, clips), jnp.int32),
            pltpu.VMEM((groups, 1, clips), jnp.int32),
            pltpu.VMEM((1, clips), jnp.int32),
            pltpu.VMEM((1, clips), jnp.int32),
        ]
        + [dma] * 8,
        compiler_params=pltpu.CompilerParams(
            collective_id=0, has_side_effects=True, vmem_limit_bytes=24 * 1024 * 1024
        ),
        cost_estimate=pl.CostEstimate(
            flops=10**9, bytes_accessed=20 * 10**6, transcendentals=0
        ),
    )(
        patch_feats.reshape(clips * patches, width),
        jnp.transpose(windows[0], (1, 2, 0)),
        counts,
        owners,
        norm_gain.reshape(1, width),
        norm_bias.reshape(1, width),
    )
    product = jnp.dot(packed, proj_weight, preferred_element_type=F32)
    result = jnp.where(live > 0.0, product + proj_bias, 0.0).astype(BF16)
    return result[None]


def solution(mesh):
    placed = (
        P("enc", "grp", None, None),
        P("enc", "grp", None, None),
        P("enc", "grp"),
        P("enc", "grp"),
        P(),
        P(),
        P(),
        P(),
    )
    return jax.shard_map(
        shards, mesh=mesh, in_specs=placed, out_specs=P("enc", "grp", None), check_vma=False
    )
```

time: 53.2 us -> 34.4 us (0.65)
  Pallas kernels: 0 us -> 22.2 us
  other arithmetic: 13.3 us -> 0.11 us
  waiting for transfers between devices: 13.1 us -> 0 us
  starting transfers between devices: 10.3 us -> 0 us
  matrix products: 9.63 us -> 7.05 us
  local copies, waits for them, and re-layouts: 6.08 us -> 4.69 us
    pallas_call x0 -> x1, Pallas kernels: none -> 22.2 us  [shards(): pl.pallas_call(functools.partial(kernel, groups, frames, per_sample, patc...]
    all_to_all x2 -> x0, starting transfers between devices: 9.01 us -> none  [the longest x1 5.2 us: shards(): lax.all_to_all(totals.reshape(groups, 1), 'grp', split_axis=0, concat_axi...]
    all_to_all x2 -> x0, waiting for transfers between devices: 6.96 us -> none  [the longest x1 6.96 us: shards(): lax.all_to_all(outgoing, 'grp', split_axis=0, concat_axis=0, tiled=True)]
    ppermute x1 -> x0, waiting for transfers between devices: 6.14 us -> none  [shifted(): return lax.ppermute(block, axis, route)]
    reduce_sum x5 -> x0, other arithmetic: 4.87 us -> none  [the longest x1 1.71 us: pool_frame(): spread = jnp.mean((values - average) ** 2, axis=-1, keepdims=True)]
    gather x4 -> x0, other arithmetic: 4.29 us -> none  [the longest x2 4.28 us: shards(): picked = sender * slot_rows + row_index - jnp.take(opening, sender)]
    unnamed x12 -> x10, local copies, waits for them, and re-layouts: 0.02 us -> 3.27 us
    gather x3 -> x0, local copies, waits for them, and re-layouts: 2.87 us -> none  [the longest x1 1.09 us: shards(): packed = jnp.take(gathered_rows, source_rows, axis=0)]
  transfers between devices with their start and end apart: 3 -> 0, of which waited for: 2 -> 0; matrix products, arithmetic and copies ran while one was open for 29% -> 0% of each run, Pallas kernels for 0% -> 0%
where the time goes in v1:
time: 34.4 us; the launch traced here: 34.1 us
  Pallas kernels  22.2 us (65%)
  matrix products  7.05 us (20%)
  local copies, waits for them, and re-layouts  4.69 us (14%)
    pallas_call x1, Pallas kernels, shards(): pl.pallas_call(functools.partial(kernel, groups, frames, per_sample, patc...  22.2 us
    dot_general x1, matrix products, shards(): product = jnp.dot(packed, proj_weight, preferred_element_type=F32)  7.05 us
    unnamed x10, local copies, waits for them, and re-layouts  3.27 us
    reshape x1, local copies, waits for them, and re-layouts, shards(): norm_gain.reshape(1, width)  0.71 us
    reshape x1, local copies, waits for them, and re-layouts, shards(): norm_bias.reshape(1, width)  0.7 us

profile of v1, /device:TPU:0, one launch (start us, length us, event | category | flops | bytes accessed | tf_op | source)
XLA Modules:
  0.0 34.1 jit_solution(7260260022420832370)
XLA Ops:
  0.0 0.0 copy-start.4
  0.0 0.7 %reshape.11.gain_ref = f32[1,1152]{1,0:T(1,128)S(1)} reshape(f32[1152]{0:T(1024)} %param.12) | data formatting | bytes 9216 | tf_op jit(solution)/shard_map/reshape | solution.py:262
  0.7 0.7 %reshape.12.bias_ref = f32[1,1152]{1,0:T(1,128)S(1)} reshape(f32[1152]{0:T(1024)} %param.13) | data formatting | bytes 9216 | tf_op jit(solution)/shard_map/reshape | solution.py:263
  1.4 0.0 copy-start
  1.4 1.3 %copy-done = bf16[1,64,8,1152]{3,2,1,0:T(8,128)(2,1)S(1)} copy-done((bf16[1,64,8,1152]{3,2,1,0:T(8,128)(2,1)S(1)}, bf16[1,64,8,1152]{3,2,1,0:T(8,128)(2,1)}, u32[]{:S(2)}) %copy-start) | copy-done | bytes 1179672
  2.7 0.0 copy-start.1
  2.7 0.7 %copy-done.1 = s32[1,64,3,4]{1,3,2,0:T(4,128)S(1)} copy-done((s32[1,64,3,4]{1,3,2,0:T(4,128)S(1)}, s32[1,64,3,4]{1,3,2,0:T(4,128)}, u32[]{:S(2)}) %copy-start.1) | copy-done | bytes 3096
  3.4 0.0 copy-start.2
  3.4 0.7 %copy-done.2 = s32[1,64]{1,0:T(1,128)S(1)} copy-done((s32[1,64]{1,0:T(1,128)S(1)}, s32[1,64]{1,0:T(1,128)}, u32[]{:S(2)}) %copy-start.2) | copy-done | bytes 280
  4.0 0.0 copy-start.3
  4.0 0.7 %copy-done.3 = s32[1,64]{1,0:T(1,128)S(1)} copy-done((s32[1,64]{1,0:T(1,128)S(1)}, s32[1,64]{1,0:T(1,128)}, u32[]{:S(2)}) %copy-start.3) | copy-done | bytes 280
  4.7 22.2 %shard_map.82 = (bf16[192,1152]{1,0:T(8,128)(2,1)S(1)}, f32[192,1]{1,0:T(8,128)S(1)}) custom-call(bf16[512,1152]{1,0:T(8,128)(2,1)S(1)} %bitcast.8, s32[3,4,64]{2,1,0:T(4,128)S(1)} %bitcast.9, s32[1,64]{1,0:T(1,128)S(1)} %copy-done.2, s32[1,64]{1,0:T(1,128)S(1)} %copy-done.3, f32[1,1152]{1,0:T(1,128)S(1)} %reshape.11.gain_ref, f32[1,1152]{1,0:T(1,128)S(1)} %reshape.12.bias_ref), custom_call_target="tpu_custom_call" | custom-call | flops 1000000000 | bytes 20000000 | tf_op jit(solution)/shard_map/pallas_call | solution.py:230
  26.9 0.1 compare_reduce_fusion
  27.0 0.0 copy-done.4
  27.0 7.0 %fusion.2 = bf16[1,192,4096]{2,1,0:T(8,128)(2,1)} fusion(bf16[192,1152]{1,0:T(8,128)(2,1)S(1)} %get-tuple-element.8, bf16[1152,4096]{1,0:T(8,128)(2,1)} %param.14, f32[4096]{0:T(1024)S(1)} %copy-done.4, pred[192]{0:T(512)(128)(4,1)S(1)} %compare_reduce_fusion), kind=kOutput, calls=%fused_computation.3 | convolution fusion | flops 1814298624 | bytes 11468992 | tf_op jit(solution)/shard_map/dot_general | solution.py:265
Async XLA Ops:
  0.0 27.0 %copy-start.4 = (f32[4096]{0:T(1024)S(1)}, f32[4096]{0:T(1024)}, u32[]{:S(2)}) copy-start(f32[4096]{0:T(1024)} %param.15) | copy-start | bytes 49156
  1.4 1.3 %copy-start = (bf16[1,64,8,1152]{3,2,1,0:T(8,128)(2,1)S(1)}, bf16[1,64,8,1152]{3,2,1,0:T(8,128)(2,1)}, u32[]{:S(2)}) copy-start(bf16[1,64,8,1152]{3,2,1,0:T(8,128)(2,1)} %param.8) | copy-start | bytes 3538948
  2.7 0.7 %copy-start.1 = (s32[1,64,3,4]{1,3,2,0:T(4,128)S(1)}, s32[1,64,3,4]{1,3,2,0:T(4,128)}, u32[]{:S(2)}) copy-start(s32[1,64,3,4]{1,3,2,0:T(4,128)} %param.9) | copy-start | bytes 9220
  3.4 0.7 %copy-start.2 = (s32[1,64]{1,0:T(1,128)S(1)}, s32[1,64]{1,0:T(1,128)}, u32[]{:S(2)}) copy-start(s32[1,64]{1,0:T(1,128)} %cnt_ref.1) | copy-start | bytes 772
  4.0 0.7 %copy-start.3 = (s32[1,64]{1,0:T(1,128)S(1)}, s32[1,64]{1,0:T(1,128)}, u32[]{:S(2)}) copy-start(s32[1,64]{1,0:T(1,128)} %own_ref.1) | copy-start | bytes 772

commit v2 on v1

--- a/solution.py
+++ b/solution.py
@@ -46,8 +46,9 @@
 
 def kernel(
     groups, frames, per_sample, patches, slot,
-    feats_ref, win_ref, cnt_ref, own_ref, gain_ref, bias_ref,
-    packed_ref, live_ref,
+    feats_hbm, win_hbm, cnt_hbm, own_hbm, gain_hbm, bias_hbm, weight_hbm,
+    packed_ref, live_ref, weight_ref,
+    feats_ref, win_ref, cnt_ref, own_ref, gain_ref, bias_ref, in_sem, feats_sem,
     normed, pooled, zsend, zrecv, outgoing, arrived,
     all_cnt, all_own, prev_cnt, prev_own,
     z_send, z_recv, a_send, a_recv, c_send, c_recv, o_send, o_recv,
@@ -74,19 +75,49 @@
         pl.semaphore_signal(barrier, inc=1, device_id=(frame + 1, me), device_id_type=MESH)
 
     step_rows = 32
-    gain, bias = gain_ref[...], bias_ref[...]
-
-    def norm_step(i):
+    pieces = 4
+    piece = feats_ref.shape[0] // pieces
+
+    def feats_copy(i):
+        at = pl.ds(i * piece, piece)
+        return pltpu.make_async_copy(feats_hbm.at[at, :], feats_ref.at[at, :], feats_sem.at[i])
+
+    small = [
+        pltpu.make_async_copy(src, dst, in_sem.at[i])
+        for i, (src, dst) in enumerate(
+            (
+                (cnt_hbm, cnt_ref),
+                (own_hbm, own_ref),
+                (gain_hbm, gain_ref),
+                (bias_hbm, bias_ref),
+                (win_hbm, win_ref),
+                (weight_hbm, weight_ref),
+            )
+        )
+    ]
+    for copy in small[:-1]:
+        copy.start()
+    for i in range(pieces):
+        feats_copy(i).start()
+    small[-1].start()
+
+    def norm_rows(i):
         at = pl.ds(pl.multiple_of(i * step_rows, step_rows), step_rows)
         values = feats_ref[at, :].astype(F32)
         centred = values - jnp.sum(values, axis=1, keepdims=True) * (1.0 / width)
         spread = jnp.sum(centred * centred, axis=1, keepdims=True) * (1.0 / width)
-        normed[at, :] = (centred * lax.rsqrt(spread + 1e-06) * gain + bias).astype(BF16)
-
-    steps = feats_ref.shape[0] // step_rows
-    early = steps // 4
-    pl.loop(0, early)(norm_step)
-
+        normed[at, :] = (
+            centred * lax.rsqrt(spread + 1e-06) * gain_ref[...].reshape(1, width)
+            + bias_ref[...].reshape(1, width)
+        ).astype(BF16)
+
+    def norm_piece(i):
+        feats_copy(i).wait()
+        per = piece // step_rows
+        pl.loop(i * per, (i + 1) * per, unroll=2)(norm_rows)
+
+    for copy in small[:4]:
+        copy.wait()
     neighbours = (frame + frames - 1) // frames + (2 * (frames - 1) - frame) // frames
     pl.semaphore_wait(barrier, groups - 1 + neighbours)
 
@@ -129,7 +160,9 @@
     all_cnt[me] = cnt_ref[...]
     all_own[me] = own_ref[...]
 
-    pl.loop(early, steps)(norm_step)
+    for i in range(pieces):
+        norm_piece(i)
+    small[4].wait()
 
     cells = clips * patches
     cell_ids = iota((clips, cells), 1)
@@ -202,6 +235,7 @@
         chosen, arrived[...].reshape(rows, width), preferred_element_type=F32
     ).astype(BF16)
 
+    small[5].wait()
     for k in order[:-1]:
         a_copy(k).wait_send()
         for copy in grp_meta(k):
@@ -227,15 +261,24 @@
     rows_out = groups * slot_rows
     block = (groups, slot, width)
     dma = pltpu.SemaphoreType.DMA((groups,))
-    packed, live = pl.pallas_call(
+    packed, live, weight = pl.pallas_call(
         functools.partial(kernel, groups, frames, per_sample, patches, slot),
         out_shape=(
             jax.ShapeDtypeStruct((rows_out, width), BF16),
             jax.ShapeDtypeStruct((rows_out, 1), F32),
+            jax.ShapeDtypeStruct(proj_weight.shape, BF16),
         ),
-        in_specs=[pl.BlockSpec(memory_space=pltpu.VMEM)] * 6,
-        out_specs=[pl.BlockSpec(memory_space=pltpu.VMEM)] * 2,
+        in_specs=[pl.BlockSpec(memory_space=pltpu.HBM)] * 7,
+        out_specs=[pl.BlockSpec(memory_space=pltpu.VMEM)] * 3,
         scratch_shapes=[
+            pltpu.VMEM((clips * patches, width), BF16),
+            pltpu.VMEM((per_sample, windows.shape[3], clips), jnp.int32),
+            pltpu.VMEM((1, clips), jnp.int32),
+            pltpu.VMEM((1, clips), jnp.int32),
+            pltpu.VMEM((width,), F32),
+            pltpu.VMEM((width,), F32),
+            pltpu.SemaphoreType.DMA((6,)),
+            pltpu.SemaphoreType.DMA((4,)),
             pltpu.VMEM((clips * patches, width), BF16),
             pltpu.VMEM((per_sample, clips, width), BF16),
             pltpu.VMEM(block, BF16),
@@ -249,20 +292,26 @@
         ]
         + [dma] * 8,
         compiler_params=pltpu.CompilerParams(
-            collective_id=0, has_side_effects=True, vmem_limit_bytes=24 * 1024 * 1024
+            collective_id=0, has_side_effects=True, vmem_limit_bytes=36 * 1024 * 1024
         ),
         cost_estimate=pl.CostEstimate(
             flops=10**9, bytes_accessed=20 * 10**6, transcendentals=0
         ),
     )(
-        patch_feats.reshape(clips * patches, width),
-        jnp.transpose(windows[0], (1, 2, 0)),
-        counts,
-        owners,
-        norm_gain.reshape(1, width),
-        norm_bias.reshape(1, width),
+        *(
+            pltpu.with_memory_space_constraint(array, pltpu.HBM)
+            for array in (
+                patch_feats.reshape(clips * patches, width),
+                jnp.transpose(windows[0], (1, 2, 0)),
+                counts,
+                owners,
+                norm_gain,
+                norm_bias,
+                proj_weight,
+            )
+        )
     )
-    product = jnp.dot(packed, proj_weight, preferred_element_type=F32)
+    product = jnp.dot(packed, weight, preferred_element_type=F32)
     result = jnp.where(live > 0.0, product + proj_bias, 0.0).astype(BF16)
     return result[None]
 

time: 34.4 us -> 25.3 us (0.74)
  local copies, waits for them, and re-layouts: 4.69 us -> 0.01 us
  matrix products: 7.05 us -> 3.37 us
  Pallas kernels: 22.2 us -> 21.7 us
    dot_general x1, matrix products: 7.05 us -> 3.37 us  [shards(): product = jnp.dot(packed, weight, preferred_element_type=F32)]
    unnamed x10 -> x2, local copies, waits for them, and re-layouts: 3.27 us -> 0.01 us
    reshape x2 -> x0, local copies, waits for them, and re-layouts: 1.41 us -> none  [the longest x1 0.71 us: shards(): norm_gain.reshape(1, width)]
    pallas_call x1, Pallas kernels: 22.2 us -> 21.7 us  [shards(): pl.pallas_call(functools.partial(kernel, groups, frames, per_sample, patc...]
where the time goes in v2:
time: 25.3 us; the launch traced here: 25.2 us
  Pallas kernels  21.7 us (86%)
  matrix products  3.37 us (13%)
    pallas_call x1, Pallas kernels, shards(): pl.pallas_call(functools.partial(kernel, groups, frames, per_sample, patc...  21.7 us
    dot_general x1, matrix products, shards(): product = jnp.dot(packed, weight, preferred_element_type=F32)  3.37 us

profile of v2, /device:TPU:0, one launch (start us, length us, event | category | flops | bytes accessed | tf_op | source)
XLA Modules:
  0.0 25.2 jit_solution(2341639455710526986)
XLA Ops:
  0.0 0.0 copy-start
  0.0 21.7 %shard_map.82 = (bf16[192,1152]{1,0:T(8,128)(2,1)S(1)}, f32[192,1]{1,0:T(8,128)S(1)}, bf16[1152,4096]{1,0:T(8,128)(2,1)S(1)}) custom-call(bf16[512,1152]{1,0:T(8,128)(2,1)} %bitcast.8, s32[3,4,64]{2,1,0:T(4,128)} %bitcast.9, s32[1,64]{1,0:T(1,128)} %cnt_hbm.1, s32[1,64]{1,0:T(1,128)} %own_hbm.1, f32[1152]{0:T(1024)} %gain_hbm.1, f32[1152]{0:T(1024)} %bias_hbm.1, ...), custom_call_target="tpu_custom_call" | custom-call | flops 1000000000 | bytes 20000000 | tf_op jit(solution)/shard_map/pallas_call | solution.py:264
  21.7 0.1 compare_reduce_fusion
  21.8 0.0 copy-done
  21.8 3.4 %fusion.2 = bf16[1,192,4096]{2,1,0:T(8,128)(2,1)} fusion(bf16[192,1152]{1,0:T(8,128)(2,1)S(1)} %get-tuple-element.9, bf16[1152,4096]{1,0:T(8,128)(2,1)S(1)} %get-tuple-element.10, f32[4096]{0:T(1024)S(1)} %copy-done, pred[192]{0:T(512)(128)(4,1)S(1)} %compare_reduce_fusion), kind=kOutput, calls=%fused_computation.3 | convolution fusion | flops 1814298624 | bytes 11468992 | tf_op jit(solution)/shard_map/dot_general | solution.py:314
Async XLA Ops:
  0.0 21.8 %copy-start = (f32[4096]{0:T(1024)S(1)}, f32[4096]{0:T(1024)}, u32[]{:S(2)}) copy-start(f32[4096]{0:T(1024)} %param.15) | copy-start | bytes 49156

commit v3 on v2

--- a/solution.py
+++ b/solution.py
@@ -31,17 +31,14 @@
     return jnp.sum(jnp.where(iota((n, n), 0) == iota((n, n), 1), row, 0.0), axis=1, keepdims=True)
 
 
-def placements(count_row, owner_row, rows, slot, per_sample):
+def placements(count_row, owner_row, slot, per_sample):
     counts, owners = count_row.astype(F32), owner_row.astype(F32)
     n = counts.shape[1]
     same = (to_column(owners) == owners) & (iota((n, n), 0) < iota((n, n), 1))
     start = jnp.sum(jnp.where(same, to_column(counts), 0.0), axis=0, keepdims=True)
     first = owners * slot + start
-    row_ids = iota((rows, n), 0).astype(F32)
-    return [
-        (row_ids == jnp.where(counts > t, first + t, -1.0)).astype(F32).astype(BF16)
-        for t in range(per_sample)
-    ]
+    targets = [jnp.where(counts > t, first + t, -1.0) for t in range(per_sample)]
+    return jnp.concatenate(targets, axis=1).astype(jnp.int32)
 
 
 def kernel(
@@ -50,7 +47,7 @@
     packed_ref, live_ref, weight_ref,
     feats_ref, win_ref, cnt_ref, own_ref, gain_ref, bias_ref, in_sem, feats_sem,
     normed, pooled, zsend, zrecv, outgoing, arrived,
-    all_cnt, all_own, prev_cnt, prev_own,
+    all_cnt, all_own, targets, prev_targets, gather,
     z_send, z_recv, a_send, a_recv, c_send, c_recv, o_send, o_recv,
 ):
     frame, me = lax.axis_index("enc"), lax.axis_index("grp")
@@ -59,20 +56,6 @@
     clips = cnt_ref.shape[1]
     rows = groups * slot
     order = list(range(groups - 1, -1, -1))
-
-    barrier = pltpu.get_barrier_semaphore()
-    for k in order[:-1]:
-        pl.semaphore_signal(
-            barrier, inc=1, device_id=(frame, partner(me, k, groups)), device_id_type=MESH
-        )
-
-    @pl.when(jnp.logical_not(first))
-    def _():
-        pl.semaphore_signal(barrier, inc=1, device_id=(frame - 1, me), device_id_type=MESH)
-
-    @pl.when(jnp.logical_not(last))
-    def _():
-        pl.semaphore_signal(barrier, inc=1, device_id=(frame + 1, me), device_id_type=MESH)
 
     step_rows = 32
     pieces = 4
@@ -101,6 +84,20 @@
         feats_copy(i).start()
     small[-1].start()
 
+    barrier = pltpu.get_barrier_semaphore()
+    for k in order[:-1]:
+        pl.semaphore_signal(
+            barrier, inc=1, device_id=(frame, partner(me, k, groups)), device_id_type=MESH
+        )
+
+    @pl.when(jnp.logical_not(first))
+    def _():
+        pl.semaphore_signal(barrier, inc=1, device_id=(frame - 1, me), device_id_type=MESH)
+
+    @pl.when(jnp.logical_not(last))
+    def _():
+        pl.semaphore_signal(barrier, inc=1, device_id=(frame + 1, me), device_id_type=MESH)
+
     def norm_rows(i):
         at = pl.ds(pl.multiple_of(i * step_rows, step_rows), step_rows)
         values = feats_ref[at, :].astype(F32)
@@ -116,61 +113,17 @@
         per = piece // step_rows
         pl.loop(i * per, (i + 1) * per, unroll=2)(norm_rows)
 
-    for copy in small[:4]:
+    for copy in small[:-1]:
         copy.wait()
-    neighbours = (frame + frames - 1) // frames + (2 * (frames - 1) - frame) // frames
-    pl.semaphore_wait(barrier, groups - 1 + neighbours)
-
-    def remote(src, dst, send, recv, k, device):
-        return pltpu.make_async_remote_copy(
-            src_ref=src, dst_ref=dst, send_sem=send.at[k], recv_sem=recv.at[k],
-            device_id=device, device_id_type=MESH,
-        )
-
-    def enc_meta():
-        to = (frame + 1, me)
-        return (
-            remote(cnt_ref, prev_cnt, c_send, c_recv, 0, to),
-            remote(own_ref, prev_own, o_send, o_recv, 0, to),
-        )
-
-    def grp_meta(k):
-        to = (frame, partner(me, k, groups))
-        return (
-            remote(cnt_ref, all_cnt.at[me], c_send, c_recv, k, to),
-            remote(own_ref, all_own.at[me], o_send, o_recv, k, to),
-        )
-
-    def z_copy(k):
-        o = partner(me, k, groups)
-        return remote(zsend.at[o], zrecv.at[o], z_send, z_recv, k, (frame - 1, me))
-
-    def a_copy(k):
-        o = partner(me, k, groups)
-        return remote(outgoing.at[o], arrived.at[me], a_send, a_recv, k, (frame, o))
-
-    @pl.when(jnp.logical_not(last))
-    def _():
-        for copy in enc_meta():
-            copy.start()
-
-    for k in order[:-1]:
-        for copy in grp_meta(k):
-            copy.start()
-    all_cnt[me] = cnt_ref[...]
-    all_own[me] = own_ref[...]
-
-    for i in range(pieces):
-        norm_piece(i)
-    small[4].wait()
+    targets[...] = placements(cnt_ref[...], own_ref[...], slot, per_sample)
 
     cells = clips * patches
+    members = win_ref.shape[1]
     cell_ids = iota((clips, cells), 1)
     base = iota((clips, 1), 0) * patches
-    members = win_ref.shape[1]
     eye = (iota((clips, clips), 0) == iota((clips, clips), 1)).astype(F32).astype(BF16)
     for t in range(per_sample):
-        picks = lax.dot_general(
+        picks = base + lax.dot_general(
             eye,
             win_ref[t].astype(F32).astype(BF16),
             (((1,), (1,)), ((), ())),
@@ -178,38 +131,67 @@
         ).astype(jnp.int32)
         chosen = jnp.zeros((clips, cells), F32)
         for w in range(members):
-            chosen += (cell_ids == base + picks[:, w : w + 1]).astype(F32)
-        total = jnp.dot(chosen.astype(BF16), normed[...], preferred_element_type=F32)
-        pooled[t] = (total * (1.0 / members)).astype(BF16)
-
-    def sort_rows(count_row, owner_row):
-        total = jnp.zeros((rows, width), F32)
-        for t, chosen in enumerate(placements(count_row, owner_row, rows, slot, per_sample)):
-            total += jnp.dot(chosen, pooled[t], preferred_element_type=F32)
+            chosen += (cell_ids == picks[:, w : w + 1]).astype(F32)
+        gather[t * clips : (t + 1) * clips, :] = chosen.astype(BF16)
+
+    neighbours = (frame + frames - 1) // frames + (2 * (frames - 1) - frame) // frames
+    pl.semaphore_wait(barrier, groups - 1 + neighbours)
+
+    def remote(src, dst, send, recv, k, device):
+        return pltpu.make_async_remote_copy(
+            src_ref=src, dst_ref=dst, send_sem=send.at[k], recv_sem=recv.at[k],
+            device_id=device, device_id_type=MESH,
+        )
+
+    def enc_meta():
+        return remote(targets, prev_targets, c_send, c_recv, 0, (frame + 1, me))
+
+    def grp_meta(k):
+        to = (frame, partner(me, k, groups))
+        return (
+            remote(cnt_ref, all_cnt.at[me], c_send, c_recv, k, to),
+            remote(own_ref, all_own.at[me], o_send, o_recv, k, to),
+        )
+
+    def z_copy(k):
+        o = partner(me, k, groups)
+        return remote(zsend.at[o], zrecv.at[o], z_send, z_recv, k, (frame - 1, me))
+
+    def a_copy(k):
+        o = partner(me, k, groups)
+        return remote(outgoing.at[o], arrived.at[me], a_send, a_recv, k, (frame, o))
+
+    @pl.when(jnp.logical_not(last))
+    def _():
+        enc_meta().start()
+
+    for k in order[:-1]:
+        for copy in grp_meta(k):
+            copy.start()
+    all_cnt[me] = cnt_ref[...]
+    all_own[me] = own_ref[...]
+
+    for i in range(pieces):
+        norm_piece(i)
+    pooled[...] = (
+        jnp.dot(gather[...], normed[...], preferred_element_type=F32) * (1.0 / members)
+    ).astype(BF16)
+
+    def sort_rows(target_row):
+        chosen = iota((rows, target_row.shape[1]), 0) == target_row
+        total = jnp.dot(
+            chosen.astype(F32).astype(BF16), pooled[...], preferred_element_type=F32
+        )
         return total.astype(BF16).reshape(groups, slot, width)
 
     @pl.when(jnp.logical_not(first))
     def _():
-        for copy in enc_meta():
-            copy.wait_recv()
-        zsend[...] = sort_rows(prev_cnt[...], prev_own[...])
+        enc_meta().wait_recv()
+        zsend[...] = sort_rows(prev_targets[...])
         for k in order:
             z_copy(k).start()
 
-    outgoing[...] = sort_rows(cnt_ref[...], own_ref[...])
-
-    for k in order:
-        o = partner(me, k, groups)
-
-        @pl.when(jnp.logical_not(last))
-        def _():
-            z_copy(k).wait_recv()
-            outgoing[o] = ((outgoing[o].astype(F32) + zrecv[o].astype(F32)) * 0.5).astype(BF16)
-
-        if k:
-            a_copy(k).start()
-        else:
-            arrived[me] = outgoing[me]
+    outgoing[...] = sort_rows(targets[...])
 
     lane = iota((1, rows), 1)
     opening, size = jnp.zeros((1, rows), F32), jnp.zeros((1, rows), F32)
@@ -229,6 +211,19 @@
     chosen = (iota((rows_out, rows), 0).astype(F32) == target).astype(F32).astype(BF16)
     live_ref[...] = (iota((rows_out, 1), 0).astype(F32) < amount).astype(F32)
 
+    for k in order:
+        o = partner(me, k, groups)
+
+        @pl.when(jnp.logical_not(last))
+        def _():
+            z_copy(k).wait_recv()
+            outgoing[o] = ((outgoing[o].astype(F32) + zrecv[o].astype(F32)) * 0.5).astype(BF16)
+
+        if k:
+            a_copy(k).start()
+        else:
+            arrived[me] = outgoing[me]
+
     for k in order[:-1]:
         a_copy(k).wait_recv()
     packed_ref[...] = jnp.dot(
@@ -248,8 +243,7 @@
 
     @pl.when(jnp.logical_not(last))
     def _():
-        for copy in enc_meta():
-            copy.wait_send()
+        enc_meta().wait_send()
 
 
 def shards(patch_feats, windows, counts, owners, norm_gain, norm_bias, proj_weight, proj_bias):
@@ -280,15 +274,16 @@
             pltpu.SemaphoreType.DMA((6,)),
             pltpu.SemaphoreType.DMA((4,)),
             pltpu.VMEM((clips * patches, width), BF16),
-            pltpu.VMEM((per_sample, clips, width), BF16),
+            pltpu.VMEM((per_sample * clips, width), BF16),
             pltpu.VMEM(block, BF16),
             pltpu.VMEM(block, BF16),
             pltpu.VMEM(block, BF16),
             pltpu.VMEM(block, BF16),
             pltpu.VMEM((groups, 1, clips), jnp.int32),
             pltpu.VMEM((groups, 1, clips), jnp.int32),
-            pltpu.VMEM((1, clips), jnp.int32),
-            pltpu.VMEM((1, clips), jnp.int32),
+            pltpu.VMEM((1, per_sample * clips), jnp.int32),
+            pltpu.VMEM((1, per_sample * clips), jnp.int32),
+            pltpu.VMEM((per_sample * clips, clips * patches), BF16),
         ]
         + [dma] * 8,
         compiler_params=pltpu.CompilerParams(

time: 25.3 us -> 24.2 us (0.957)
  Pallas kernels: 21.7 us -> 20.6 us
    pallas_call x1, Pallas kernels: 21.7 us -> 20.6 us  [shards(): pl.pallas_call(functools.partial(kernel, groups, frames, per_sample, patc...]
where the time goes in v3:
time: 24.2 us; the launch traced here: 24.1 us
  Pallas kernels  20.6 us (85%)
  matrix products  3.37 us (14%)
    pallas_call x1, Pallas kernels, shards(): pl.pallas_call(functools.partial(kernel, groups, frames, per_sample, patc...  20.6 us
    dot_general x1, matrix products, shards(): product = jnp.dot(packed, weight, preferred_element_type=F32)  3.37 us

profile of v3, /device:TPU:0, one launch (start us, length us, event | category | flops | bytes accessed | tf_op | source)
XLA Modules:
  0.0 24.1 jit_solution(2529924429452288393)
XLA Ops:
  0.0 0.0 copy-start
  0.0 20.6 %shard_map.82 = (bf16[192,1152]{1,0:T(8,128)(2,1)S(1)}, f32[192,1]{1,0:T(8,128)S(1)}, bf16[1152,4096]{1,0:T(8,128)(2,1)S(1)}) custom-call(bf16[512,1152]{1,0:T(8,128)(2,1)} %bitcast.8, s32[3,4,64]{2,1,0:T(4,128)} %bitcast.9, s32[1,64]{1,0:T(1,128)} %cnt_hbm.1, s32[1,64]{1,0:T(1,128)} %own_hbm.1, f32[1152]{0:T(1024)} %gain_hbm.1, f32[1152]{0:T(1024)} %bias_hbm.1, ...), custom_call_target="tpu_custom_call" | custom-call | flops 1000000000 | bytes 20000000 | tf_op jit(solution)/shard_map/pallas_call | solution.py:258
  20.6 0.1 compare_reduce_fusion
  20.7 0.0 copy-done
  20.7 3.4 %fusion.2 = bf16[1,192,4096]{2,1,0:T(8,128)(2,1)} fusion(bf16[192,1152]{1,0:T(8,128)(2,1)S(1)} %get-tuple-element.9, bf16[1152,4096]{1,0:T(8,128)(2,1)S(1)} %get-tuple-element.10, f32[4096]{0:T(1024)S(1)} %copy-done, pred[192]{0:T(512)(128)(4,1)S(1)} %compare_reduce_fusion), kind=kOutput, calls=%fused_computation.3 | convolution fusion | flops 1814298624 | bytes 11468992 | tf_op jit(solution)/shard_map/dot_general | solution.py:309
Async XLA Ops:
  0.0 20.7 %copy-start = (f32[4096]{0:T(1024)S(1)}, f32[4096]{0:T(1024)}, u32[]{:S(2)}) copy-start(f32[4096]{0:T(1024)} %param.15) | copy-start | bytes 49156

commit v4 on v3

--- a/solution.py
+++ b/solution.py
@@ -82,7 +82,6 @@
         copy.start()
     for i in range(pieces):
         feats_copy(i).start()
-    small[-1].start()
 
     barrier = pltpu.get_barrier_semaphore()
     for k in order[:-1]:
@@ -111,12 +110,51 @@
     def norm_piece(i):
         feats_copy(i).wait()
         per = piece // step_rows
-        pl.loop(i * per, (i + 1) * per, unroll=2)(norm_rows)
-
-    for copy in small[:-1]:
+        pl.loop(i * per, (i + 1) * per, unroll=4)(norm_rows)
+
+    for copy in small[:2]:
         copy.wait()
     targets[...] = placements(cnt_ref[...], own_ref[...], slot, per_sample)
 
+    neighbours = (frame + frames - 1) // frames + (2 * (frames - 1) - frame) // frames
+    pl.semaphore_wait(barrier, groups - 1 + neighbours)
+
+    def remote(src, dst, send, recv, k, device):
+        return pltpu.make_async_remote_copy(
+            src_ref=src, dst_ref=dst, send_sem=send.at[k], recv_sem=recv.at[k],
+            device_id=device, device_id_type=MESH,
+        )
+
+    def enc_meta():
+        return remote(targets, prev_targets, c_send, c_recv, 0, (frame + 1, me))
+
+    def grp_meta(k):
+        to = (frame, partner(me, k, groups))
+        return (
+            remote(cnt_ref, all_cnt.at[me], c_send, c_recv, k, to),
+            remote(own_ref, all_own.at[me], o_send, o_recv, k, to),
+        )
+
+    def z_copy(k):
+        o = partner(me, k, groups)
+        return remote(zsend.at[o], zrecv.at[o], z_send, z_recv, k, (frame - 1, me))
+
+    def a_copy(k):
+        o = partner(me, k, groups)
+        return remote(outgoing.at[o], arrived.at[me], a_send, a_recv, k, (frame, o))
+
+    @pl.when(jnp.logical_not(last))
+    def _():
+        enc_meta().start()
+
+    for k in order[:-1]:
+        for copy in grp_meta(k):
+            copy.start()
+    all_cnt[me] = cnt_ref[...]
+    all_own[me] = own_ref[...]
+
+    for copy in small[2:5]:
+        copy.wait()
     cells = clips * patches
     members = win_ref.shape[1]
     cell_ids = iota((clips, cells), 1)
@@ -134,45 +172,9 @@
             chosen += (cell_ids == picks[:, w : w + 1]).astype(F32)
         gather[t * clips : (t + 1) * clips, :] = chosen.astype(BF16)
 
-    neighbours = (frame + frames - 1) // frames + (2 * (frames - 1) - frame) // frames
-    pl.semaphore_wait(barrier, groups - 1 + neighbours)
-
-    def remote(src, dst, send, recv, k, device):
-        return pltpu.make_async_remote_copy(
-            src_ref=src, dst_ref=dst, send_sem=send.at[k], recv_sem=recv.at[k],
-            device_id=device, device_id_type=MESH,
-        )
-
-    def enc_meta():
-        return remote(targets, prev_targets, c_send, c_recv, 0, (frame + 1, me))
-
-    def grp_meta(k):
-        to = (frame, partner(me, k, groups))
-        return (
-            remote(cnt_ref, all_cnt.at[me], c_send, c_recv, k, to),
-            remote(own_ref, all_own.at[me], o_send, o_recv, k, to),
-        )
-
-    def z_copy(k):
-        o = partner(me, k, groups)
-        return remote(zsend.at[o], zrecv.at[o], z_send, z_recv, k, (frame - 1, me))
-
-    def a_copy(k):
-        o = partner(me, k, groups)
-        return remote(outgoing.at[o], arrived.at[me], a_send, a_recv, k, (frame, o))
-
-    @pl.when(jnp.logical_not(last))
-    def _():
-        enc_meta().start()
-
-    for k in order[:-1]:
-        for copy in grp_meta(k):
-            copy.start()
-    all_cnt[me] = cnt_ref[...]
-    all_own[me] = own_ref[...]
-
     for i in range(pieces):
         norm_piece(i)
+    small[5].start()
     pooled[...] = (
         jnp.dot(gather[...], normed[...], preferred_element_type=F32) * (1.0 / members)
     ).astype(BF16)

time: 24.2 us -> 23.9 us (0.988)
  Pallas kernels: 20.6 us -> 20.3 us
    pallas_call x1, Pallas kernels: 20.6 us -> 20.3 us  [shards(): pl.pallas_call(functools.partial(kernel, groups, frames, per_sample, patc...]
where the time goes in v4:
time: 23.9 us; the launch traced here: 23.8 us
  Pallas kernels  20.3 us (85%)
  matrix products  3.37 us (14%)
    pallas_call x1, Pallas kernels, shards(): pl.pallas_call(functools.partial(kernel, groups, frames, per_sample, patc...  20.3 us
    dot_general x1, matrix products, shards(): product = jnp.dot(packed, weight, preferred_element_type=F32)  3.37 us

profile of v4, /device:TPU:0, one launch (start us, length us, event | category | flops | bytes accessed | tf_op | source)
XLA Modules:
  0.0 23.8 jit_solution(5567554069992419307)
XLA Ops:
  0.0 0.0 copy-start
  0.0 20.3 %shard_map.82 = (bf16[192,1152]{1,0:T(8,128)(2,1)S(1)}, f32[192,1]{1,0:T(8,128)S(1)}, bf16[1152,4096]{1,0:T(8,128)(2,1)S(1)}) custom-call(bf16[512,1152]{1,0:T(8,128)(2,1)} %bitcast.8, s32[3,4,64]{2,1,0:T(4,128)} %bitcast.9, s32[1,64]{1,0:T(1,128)} %cnt_hbm.1, s32[1,64]{1,0:T(1,128)} %own_hbm.1, f32[1152]{0:T(1024)} %gain_hbm.1, f32[1152]{0:T(1024)} %bias_hbm.1, ...), custom_call_target="tpu_custom_call" | custom-call | flops 1000000000 | bytes 20000000 | tf_op jit(solution)/shard_map/pallas_call | solution.py:260
  20.3 0.1 compare_reduce_fusion
  20.4 0.0 copy-done
  20.4 3.4 %fusion.2 = bf16[1,192,4096]{2,1,0:T(8,128)(2,1)} fusion(bf16[192,1152]{1,0:T(8,128)(2,1)S(1)} %get-tuple-element.9, bf16[1152,4096]{1,0:T(8,128)(2,1)S(1)} %get-tuple-element.10, f32[4096]{0:T(1024)S(1)} %copy-done, pred[192]{0:T(512)(128)(4,1)S(1)} %compare_reduce_fusion), kind=kOutput, calls=%fused_computation.3 | convolution fusion | flops 1814298624 | bytes 11468992 | tf_op jit(solution)/shard_map/dot_general | solution.py:311
Async XLA Ops:
  0.0 20.4 %copy-start = (f32[4096]{0:T(1024)S(1)}, f32[4096]{0:T(1024)}, u32[]{:S(2)}) copy-start(f32[4096]{0:T(1024)} %param.15) | copy-start | bytes 49156
